TPU v7x, 32 devices: a whole 2x2x4 slice. The times are simulated.
32 devices in a mesh: dp: 4 (over y, core), expert: 4 (over z), tensor: 2 (over x).
Axes of the slice: x: 2, y: 2, z: 4, core: 2. Of those that a mesh axis runs over, the one named last changes fastest.
Arguments:
- router_input: bfloat16 [1024, 2048], P(('dp', 'expert'), 'tensor'), may hold values from -6 to 6
- router_weight: bfloat16 [2048, 8], replicated, may hold values from -0.125 to 0.125
- expert_ids: int32 [1024, 2], P(('dp', 'expert', 'tensor')), may hold values from 0 to 7, all different within a row; in each aligned block of 32 rows (0 to 31, 32 to 63, ...) at most 9 rows name the same one
- down_weight: bfloat16 [61440, 2048], P(('expert', 'tensor')), may hold values from -0.0625 to 0.0625
- hidden: bfloat16 [4, 72, 61440], P('dp', None, ('expert', 'tensor')), may hold values from -6 to 6
- grad_output: bfloat16 [1024, 2048], P(('dp', 'expert', 'tensor')), may hold values from -4 to 4
Outputs:
- weight_grad: bfloat16 [61440, 2048], P(('expert', 'tensor', 'dp'))
- hidden_grad: bfloat16 [4, 72, 61440], P('dp', None, ('expert', 'tensor'))
- router_grad: float32 [2048, 8], replicated
- input_grad: bfloat16 [1024, 2048], P(('dp', 'expert', 'tensor'))
Inputs may be any that keep to these rules, and one draw needn't show every extreme that they name: `expert_ids`: each row names 2 different experts. Within the 32 rows of one device no expert is named more than 9 times, and some device's rows name some expert exactly 9 times.
All inputs are finite; a program needn't handle non-finite values.
Results may differ from a plain program's by a relative error of at most 0.018.
Values may be sent and summed in bfloat16 or wider, within the bound.
A program may use at most 192 MiB of HBM per device.

v0:
```python
import jax
import jax.numpy as jnp
from jax import lax
from jax.sharding import PartitionSpec as P


def per_device(router_input, router_weight, expert_ids, down_weight, hidden, grad_output):
    token_rows = grad_output.shape[0]
    model_width = grad_output.shape[1]
    expert_count = router_weight.shape[1]
    choose_count = expert_ids.shape[1]
    expert_ranks = lax.axis_size("expert")
    tensor_ranks = lax.axis_size("tensor")
    sources = expert_ranks * tensor_ranks
    spread = sources // expert_count
    capacity = hidden.shape[1] // sources
    full_input = lax.all_to_all(router_input, "tensor", split_axis=0, concat_axis=1, tiled=True)
    logits = jnp.dot(full_input, router_weight, preferred_element_type=jnp.float32)
    labels = jnp.arange(expert_count, dtype=jnp.int32)
    onehot_int = (expert_ids[:, :, None] == labels).astype(jnp.int32)
    onehot = onehot_int.astype(jnp.float32)
    picked = jnp.sum(onehot * logits[:, None, :], axis=2)
    first_gate = jax.nn.sigmoid(picked[:, 0] - picked[:, 1])
    second_gate = jax.nn.sigmoid(picked[:, 1] - picked[:, 0])
    gate_values = jnp.stack([first_gate, second_gate], axis=1)
    gate_low = gate_values.astype(jnp.bfloat16)
    flat_hits = onehot_int.reshape(token_rows * choose_count, expert_count)
    before = jnp.cumsum(flat_hits, axis=0) - flat_hits
    slot_pos = jnp.sum(before * flat_hits, axis=1).reshape(token_rows, choose_count)
    slot_ids = jnp.arange(capacity, dtype=jnp.int32)
    dispatch_table = onehot[:, :, :, None] * (slot_pos[:, :, None, None] == slot_ids).astype(
        jnp.float32
    )
    slot_table = jnp.sum(dispatch_table, axis=1).astype(jnp.bfloat16)
    packed_grad = jnp.einsum(
        "rec,rd->ecd", slot_table, grad_output, preferred_element_type=jnp.float32
    ).astype(jnp.bfloat16)
    packed_gate = jnp.einsum("rkec,rk->ec", dispatch_table, gate_low.astype(jnp.float32)).astype(
        jnp.bfloat16
    )
    send_grad = jnp.repeat(packed_grad, spread, axis=0)
    send_gate = jnp.repeat(packed_gate, spread, axis=0)
    recv_grad, recv_gate = (
        lax.all_to_all(send_grad, ("expert", "tensor"), split_axis=0, concat_axis=0, tiled=True),
        lax.all_to_all(send_gate, ("expert", "tensor"), split_axis=0, concat_axis=0, tiled=True),
    )
    recv_grad = recv_grad.reshape(sources * capacity, model_width)
    recv_gate = recv_gate.reshape(sources * capacity).astype(jnp.float32)
    hidden_rows = hidden[0]
    gated_grad = (recv_gate[:, None] * recv_grad.astype(jnp.float32)).astype(jnp.bfloat16)
    expert_image = lax.dot_general(
        recv_grad, down_weight, (((1,), (1,)), ((), ())), preferred_element_type=jnp.float32
    )
    hidden_part = (recv_gate[:, None] * expert_image).astype(jnp.bfloat16)
    gate_partial = jnp.sum(hidden_rows.astype(jnp.float32) * expert_image, axis=1).reshape(
        sources, capacity
    )
    returned = lax.all_to_all(
        gate_partial, ("expert", "tensor"), split_axis=0, concat_axis=0, tiled=True
    )
    expert_sums = jnp.sum(returned.reshape(expert_count, spread, capacity), axis=1)
    gate_grad = jnp.einsum("rkec,ec->rk", dispatch_table, expert_sums)
    mixed_term = jnp.sum(gate_values * gate_grad, axis=1, keepdims=True)
    logit_part = gate_values * (gate_grad - mixed_term)
    logit_grad = jnp.sum(onehot * logit_part[:, :, None], axis=1)
    input_grad = jnp.dot(
        logit_grad, router_weight.astype(jnp.float32).T, precision=lax.Precision.HIGHEST
    ).astype(jnp.bfloat16)
    router_local = jnp.dot(
        full_input.astype(jnp.float32).T, logit_grad, precision=lax.Precision.HIGHEST
    )
    router_grad = lax.psum(router_local, ("dp", "expert", "tensor"))
    hidden_all = lax.all_to_all(hidden_rows, "dp", split_axis=1, concat_axis=0, tiled=True)
    gated_all = lax.all_gather(gated_grad, "dp", axis=0, tiled=True)
    weight_sum = lax.dot_general(
        hidden_all, gated_all, (((0,), (0,)), ((), ())), preferred_element_type=jnp.float32
    ).astype(jnp.bfloat16)
    return (weight_sum, hidden_part[None], router_grad, input_grad)


def solution(mesh):
    return jax.shard_map(
        per_device,
        mesh=mesh,
        in_specs=(
            P(("dp", "expert"), "tensor"),
            P(),
            P(("dp", "expert", "tensor"), None),
            P(("expert", "tensor"), None),
            P("dp", None, ("expert", "tensor")),
            P(("dp", "expert", "tensor"), None),
        ),
        out_specs=(
            P(("expert", "tensor", "dp"), None),
            P("dp", None, ("expert", "tensor")),
            P(),
            P(("dp", "expert", "tensor"), None),
        ),
        check_vma=False,
    )
```

profile of v0, /device:TPU:1, one launch (start us, length us, event | category | flops | bytes accessed | tf_op | source)
XLA Modules:
  0.0 211.5 jit_solution(2945085626296198110)
XLA Ops:
  8.0 3.5 %all-to-all-start = ((bf16[2,32,1024]{2,1,0:T(8,128)(2,1)}), bf16[2,32,1024]{2,1,0:T(8,128)(2,1)S(1)}, u32[]{:S(2)}, u32[]{:S(2)}) async-start(bf16[2,32,1024]{2,1,0:T(8,128)(2,1)} %bitcast.51), calls=%async_computation | async-start | bytes 262144 | tf_op jit(solution)/shard_map/all_to_all | solution.py:17
  11.5 0.8 copy.34
  12.3 0.7 convert_convert_fusion
  13.2 0.1 reduce_window_sum.11
  13.3 0.2 select_reduce_fusion
  13.4 0.1 eq.53
  13.7 1.7 all-to-all-done
  15.4 0.9 fusion.14
  16.3 0.7 multiply_reduce_fusion.2
  17.1 0.2 fusion.2
  17.4 0.6 copy.37
  18.0 4.9 %all-to-all-start.1 = ((bf16[8,1,9]{2,1,0:T(2,128)(2,1)}), bf16[8,1,9]{2,1,0:T(2,128)(2,1)S(1)}, u32[]{:S(2)}, u32[]{:S(2)}) async-start(bf16[8,1,9]{2,1,0:T(2,128)(2,1)} %copy.37), calls=%async_computation.1 | async-start | bytes 8192 | tf_op jit(solution)/shard_map/all_to_all | solution.py:45
  22.8 1.1 convolution_convert_fusion
  23.9 4.2 %all-to-all-done.1 = bf16[8,1,9]{2,1,0:T(2,128)(2,1)S(1)} async-done(((bf16[8,1,9]{2,1,0:T(2,128)(2,1)}), bf16[8,1,9]{2,1,0:T(2,128)(2,1)S(1)}, u32[]{:S(2)}, u32[]{:S(2)}) %all-to-all-start.1) | async-done | bytes 176 | tf_op jit(solution)/shard_map/all_to_all | solution.py:45
  28.1 3.5 %all-to-all-start.2 = ((bf16[8,9,2048]{2,1,0:T(8,128)(2,1)}), bf16[8,9,2048]{2,1,0:T(8,128)(2,1)S(1)}, u32[]{:S(2)}, u32[]{:S(2)}) async-start(bf16[8,9,2048]{2,1,0:T(8,128)(2,1)} %convolution_convert_fusion), calls=%async_computation.2 | async-start | bytes 1048576 | tf_op jit(solution)/shard_map/all_to_all | solution.py:44
  31.7 10.3 %all-to-all-done.2 = bf16[8,9,2048]{2,1,0:T(8,128)(2,1)S(1)} async-done(((bf16[8,9,2048]{2,1,0:T(8,128)(2,1)}), bf16[8,9,2048]{2,1,0:T(8,128)(2,1)S(1)}, u32[]{:S(2)}, u32[]{:S(2)}) %all-to-all-start.2) | async-done | bytes 294944 | tf_op jit(solution)/shard_map/all_to_all | solution.py:44
  42.0 0.1 reshape.60
  42.2 0.8 multiply_convert_fusion.1
  43.0 15.7 %fusion = (f32[72]{0:T(128)S(1)}, bf16[1,72,7680]{2,1,0:T(8,128)(2,1)}) fusion(bf16[1,72,7680]{2,1,0:T(8,128)(2,1)S(1)} %copy-done.1, f32[72]{0:T(128)S(1)} %reshape.61, bf16[72,2048]{1,0:T(8,128)(2,1)S(1)} %reshape.60, bf16[7680,2048]{1,0:T(8,128)(2,1)} %param.9), kind=kOutput, calls=%fused_computation.5 | convolution fusion | flops 2267688960 | bytes 33964608 | tf_op jit(solution)/shard_map/dot_general | solution.py:51
  58.8 0.7 all_to_all.54
  59.5 6.6 %all-to-all-start.4 = ((f32[8,1,9]{2,1,0:T(1,128)}), f32[8,1,9]{2,1,0:T(1,128)S(1)}, u32[]{:S(2)}, u32[]{:S(2)}) async-start(f32[8,1,9]{2,1,0:T(1,128)} %bitcast.13), calls=%async_computation.4 | async-start | bytes 8192 | tf_op jit(solution)/shard_map/all_to_all | solution.py:58
  66.0 0.3 all_to_all.50
  66.4 1.1 copy.39
  67.5 3.8 %all-to-all-done.4 = f32[8,1,9]{2,1,0:T(1,128)S(1)} async-done(((f32[8,1,9]{2,1,0:T(1,128)}), f32[8,1,9]{2,1,0:T(1,128)S(1)}, u32[]{:S(2)}, u32[]{:S(2)}) %all-to-all-start.4) | async-done | bytes 320 | tf_op jit(solution)/shard_map/all_to_all | solution.py:58
  71.3 6.7 %all-to-all-start.3 = ((bf16[72,4,1920]{2,0,1:T(8,128)(2,1)}), bf16[72,4,1920]{2,0,1:T(8,128)(2,1)S(1)}, u32[]{:S(2)}, u32[]{:S(2)}) async-start(bf16[72,4,1920]{2,0,1:T(8,128)(2,1)} %copy.39), calls=%async_computation.3 | async-start | bytes 2211840 | tf_op jit(solution)/shard_map/all_to_all | solution.py:73
  78.2 0.8 convolution_bitcast_fusion
  79.1 1.0 convolution_convert_fusion.1
  80.0 12.1 %all-to-all-done.3 = bf16[72,4,1920]{2,0,1:T(8,128)(2,1)S(1)} async-done(((bf16[72,4,1920]{2,0,1:T(8,128)(2,1)}), bf16[72,4,1920]{2,0,1:T(8,128)(2,1)S(1)}, u32[]{:S(2)}, u32[]{:S(2)}) %all-to-all-start.3) | async-done | bytes 1105952 | tf_op jit(solution)/shard_map/all_to_all | solution.py:73
  92.1 8.0 %convert_bitcast_fusion = bf16[1920,2048]{0,1:T(8,128)(2,1)} fusion(bf16[288,2048]{1,0:T(8,128)(2,1)} %all-gather.2.cloned.1.call-done, bf16[288,1920]{1,0:T(8,128)(2,1)S(1)} %bitcast.49), kind=kOutput, calls=%fused_computation | convolution fusion | flops 2268856320 | bytes 10149888 | tf_op jit(solution)/shard_map/dot_general | solution.py:75
  100.1 10.6 %copy.41 = bf16[1920,2048]{1,0:T(8,128)(2,1)} copy(bf16[1920,2048]{0,1:T(8,128)(2,1)} %convert_bitcast_fusion) | data formatting | bytes 15728640
  110.7 91.9 %all-reduce.2.cloned.1.call-done = f32[2048,8]{0,1:T(8,128)} async-done(((f32[2048,8]{0,1:T(8,128)}), f32[2048,8]{0,1:T(8,128)}) %all-reduce.2.cloned.1.call-update) | async-done | bytes 65552 | tf_op jit(solution)/shard_map/psum | solution.py:72
  202.5 1.5 copy.56
  (30 shorter events, 0.8 us)
Async XLA Ops:
  8.0 14.8 %copy-start = (bf16[32,2048]{1,0:T(8,128)(2,1)S(1)}, bf16[32,2048]{1,0:T(8,128)(2,1)}, u32[]{:S(2)}) copy-start(bf16[32,2048]{1,0:T(8,128)(2,1)} %param.11) | copy-start | bytes 393220
  8.0 7.4 %all-to-all-start = ((bf16[2,32,1024]{2,1,0:T(8,128)(2,1)}), bf16[2,32,1024]{2,1,0:T(8,128)(2,1)S(1)}, u32[]{:S(2)}, u32[]{:S(2)}) async-start(bf16[2,32,1024]{2,1,0:T(8,128)(2,1)} %bitcast.51), calls=%async_computation | async-start | bytes 262144 | tf_op jit(solution)/shard_map/all_to_all | solution.py:17
  18.0 10.1 %all-to-all-start.1 = ((bf16[8,1,9]{2,1,0:T(2,128)(2,1)}), bf16[8,1,9]{2,1,0:T(2,128)(2,1)S(1)}, u32[]{:S(2)}, u32[]{:S(2)}) async-start(bf16[8,1,9]{2,1,0:T(2,128)(2,1)} %copy.37), calls=%async_computation.1 | async-start | bytes 8192 | tf_op jit(solution)/shard_map/all_to_all | solution.py:45
  23.9 19.1 %copy-start.1 = (bf16[1,72,7680]{2,1,0:T(8,128)(2,1)S(1)}, bf16[1,72,7680]{2,1,0:T(8,128)(2,1)}, u32[]{:S(2)}) copy-start(bf16[1,72,7680]{2,1,0:T(8,128)(2,1)} %param.10) | copy-start | bytes 3317764
  28.1 13.9 %all-to-all-start.2 = ((bf16[8,9,2048]{2,1,0:T(8,128)(2,1)}), bf16[8,9,2048]{2,1,0:T(8,128)(2,1)S(1)}, u32[]{:S(2)}, u32[]{:S(2)}) async-start(bf16[8,9,2048]{2,1,0:T(8,128)(2,1)} %convolution_convert_fusion), calls=%async_computation.2 | async-start | bytes 1048576 | tf_op jit(solution)/shard_map/all_to_all | solution.py:44
  31.6 60.5 %all-gather.2.cloned.1.call-start = ((), (), s32[]{:S(2)}) async-start(), calls=%async_computation.5 | async-start | bytes 1474560 | tf_op jit(solution)/shard_map/all_gather | solution.py:74
  59.5 11.9 %all-to-all-start.4 = ((f32[8,1,9]{2,1,0:T(1,128)}), f32[8,1,9]{2,1,0:T(1,128)S(1)}, u32[]{:S(2)}, u32[]{:S(2)}) async-start(f32[8,1,9]{2,1,0:T(1,128)} %bitcast.13), calls=%async_computation.4 | async-start | bytes 8192 | tf_op jit(solution)/shard_map/all_to_all | solution.py:58
  67.5 10.7 %copy-start.3 = (s32[32,2]{0,1:T(2,128)S(1)}, s32[32,2]{0,1:T(2,128)}, u32[]{:S(2)}) copy-start(s32[32,2]{0,1:T(2,128)} %param.8) | copy-start | bytes 772
  67.5 11.6 %copy-start.2 = (bf16[2048,8]{0,1:T(8,128)(2,1)S(1)}, bf16[2048,8]{0,1:T(8,128)(2,1)}, u32[]{:S(2)}) copy-start(bf16[2048,8]{0,1:T(8,128)(2,1)} %param.7) | copy-start | bytes 98308
  71.3 20.8 %all-to-all-start.3 = ((bf16[72,4,1920]{2,0,1:T(8,128)(2,1)}), bf16[72,4,1920]{2,0,1:T(8,128)(2,1)S(1)}, u32[]{:S(2)}, u32[]{:S(2)}) async-start(bf16[72,4,1920]{2,0,1:T(8,128)(2,1)} %copy.39), calls=%async_computation.3 | async-start | bytes 2211840 | tf_op jit(solution)/shard_map/all_to_all | solution.py:73
  78.0 124.6 %all-reduce.2.cloned.1.call-start = ((), (), s32[]{:S(2)}) async-start(), calls=%async_computation.6 | async-start | bytes 131072 | tf_op jit(solution)/shard_map/psum | solution.py:72
Sparse Core Ops, SparseCore 0:
  43.1 21.1 all-gather.1
Sparse Core Ops, SparseCore 1:
  84.6 117.9 all-reduce.1
where the time goes:
time: 212 us; the launch traced here: 211 us
  waiting for transfers between devices  124 us (58%)
  matrix products  27.6 us (13%)
  starting transfers between devices  25.2 us (12%)
  local copies, waits for them, and re-layouts  16.3 us (8%)
  between operations  15.6 us (7%)
  other arithmetic  2.78 us (1%)
    psum x1, waiting for transfers between devices, per_device(): router_grad = lax.psum(router_local, ('dp', 'expert', 'tensor'))  91.9 us
    dot_general x1, matrix products, per_device(): lax.dot_general(recv_grad, down_weight, (((1,), (1,)), ((), ())), preferr...  15.7 us
    unnamed x12, local copies, waits for them, and re-layouts  13 us
    all_to_all x1, waiting for transfers between devices, per_device(): lax.all_to_all(hidden_rows, 'dp', split_axis=1, concat_axis=0, tiled=True)  12.1 us
    all_to_all x1, waiting for transfers between devices, per_device(): lax.all_to_all(send_grad, ('expert', 'tensor'), split_axis=0, concat_axis...  10.3 us
    dot_general x1, matrix products, per_device(): lax.dot_general(hidden_all, gated_all, (((0,), (0,)), ((), ())), preferre...  7.96 us
    all_to_all x1, starting transfers between devices, per_device(): lax.all_to_all(hidden_rows, 'dp', split_axis=1, concat_axis=0, tiled=True)  6.66 us
    all_to_all x1, starting transfers between devices, per_device(): lax.all_to_all(gate_partial, ('expert', 'tensor'), split_axis=0, concat_a...  6.6 us
  transfers between devices with their start and end apart: 7, of which 6 were waited for; matrix products, arithmetic and copies ran while one was open for 19% of the time, Pallas kernels for 0%

commit v1 on v0

--- a/solution.py
+++ b/solution.py
@@ -69,7 +69,8 @@
     router_local = jnp.dot(
         full_input.astype(jnp.float32).T, logit_grad, precision=lax.Precision.HIGHEST
     )
-    router_grad = lax.psum(router_local, ("dp", "expert", "tensor"))
+    parts = lax.all_gather(router_local, ("dp", "expert", "tensor"), axis=0, tiled=False)
+    router_grad = parts.sum(axis=0)
     hidden_all = lax.all_to_all(hidden_rows, "dp", split_axis=1, concat_axis=0, tiled=True)
     gated_all = lax.all_gather(gated_grad, "dp", axis=0, tiled=True)
     weight_sum = lax.dot_general(

time: 212 us -> 138 us (0.65)
  waiting for transfers between devices: 124 us -> 45.4 us
  blocking collectives: 0 us -> 11.7 us
  starting transfers between devices: 25.2 us -> 18.6 us
  other arithmetic: 2.78 us -> 5.11 us
    psum x1 -> x0, waiting for transfers between devices: 91.9 us -> none  [per_device(): router_grad = lax.psum(router_local, ('dp', 'expert', 'tensor'))]
    all_gather x0 -> x1, waiting for transfers between devices: none -> 15.5 us  [per_device(): lax.all_gather(router_local, ('dp', 'expert', 'tensor'), axis=0, tiled=Fa...]
    all_to_all x0 -> x1, blocking collectives: none -> 11.7 us  [per_device(): lax.all_to_all(gate_partial, ('expert', 'tensor'), split_axis=0, concat_a...]
    all_to_all x1 -> x0, starting transfers between devices: 6.6 us -> none  [per_device(): lax.all_to_all(gate_partial, ('expert', 'tensor'), split_axis=0, concat_a...]
    all_to_all x1 -> x0, waiting for transfers between devices: 3.84 us -> none  [per_device(): lax.all_to_all(gate_partial, ('expert', 'tensor'), split_axis=0, concat_a...]
    reduce_sum x0 -> x1, other arithmetic: none -> 2.33 us  [per_device(): router_grad = parts.sum(axis=0)]
    unnamed x12 -> x11, local copies, waits for them, and re-layouts: 13 us -> 11.5 us
  transfers between devices with their start and end apart: 7 -> 6, of which waited for: 6 -> 5; matrix products, arithmetic and copies ran while one was open for 19% -> 30% of each run, Pallas kernels for 0% -> 0%
where the time goes in v1:
time: 138 us; the launch traced here: 137 us
  waiting for transfers between devices  45.4 us (33%)
  matrix products  27.6 us (20%)
  starting transfers between devices  18.6 us (13%)
  local copies, waits for them, and re-layouts  14.2 us (10%)
  between operations  14.2 us (10%)
  blocking collectives  11.7 us (8%)
  other arithmetic  5.11 us (4%)
    dot_general x1, matrix products, per_device(): lax.dot_general(recv_grad, down_weight, (((1,), (1,)), ((), ())), preferr...  15.7 us
    all_gather x1, waiting for transfers between devices, per_device(): lax.all_gather(router_local, ('dp', 'expert', 'tensor'), axis=0, tiled=Fa...  15.5 us
    all_to_all x1, waiting for transfers between devices, per_device(): lax.all_to_all(hidden_rows, 'dp', split_axis=1, concat_axis=0, tiled=True)  13.6 us
    all_to_all x1, blocking collectives, per_device(): lax.all_to_all(gate_partial, ('expert', 'tensor'), split_axis=0, concat_a...  11.7 us
    unnamed x11, local copies, waits for them, and re-layouts  11.5 us
    all_to_all x1, waiting for transfers between devices, per_device(): lax.all_to_all(send_grad, ('expert', 'tensor'), split_axis=0, concat_axis...  10.3 us
    dot_general x1, matrix products, per_device(): lax.dot_general(hidden_all, gated_all, (((0,), (0,)), ((), ())), preferre...  7.96 us
    all_to_all x1, starting transfers between devices, per_device(): lax.all_to_all(hidden_rows, 'dp', split_axis=1, concat_axis=0, tiled=True)  6.66 us
  transfers between devices with their start and end apart: 6, of which 5 were waited for; matrix products, arithmetic and copies ran while one was open for 30% of the time, Pallas kernels for 0%

profile of v1, /device:TPU:1, one launch (start us, length us, event | category | flops | bytes accessed | tf_op | source)
XLA Modules:
  0.0 136.9 jit_solution(5524990726157091216)
XLA Ops:
  7.2 3.5 %all-to-all-start = ((bf16[2,32,1024]{2,1,0:T(8,128)(2,1)}), bf16[2,32,1024]{2,1,0:T(8,128)(2,1)S(1)}, u32[]{:S(2)}, u32[]{:S(2)}) async-start(bf16[2,32,1024]{2,1,0:T(8,128)(2,1)} %bitcast.53), calls=%async_computation | async-start | bytes 262144 | tf_op jit(solution)/shard_map/all_to_all | solution.py:17
  10.7 0.8 copy.34
  11.5 0.7 convert_convert_fusion
  12.2 0.1 eq.49
  12.3 0.1 reduce_window_sum.11
  12.4 0.2 select_reduce_fusion
  12.6 0.1 eq.53
  12.8 1.7 %all-to-all-done = bf16[2,32,1024]{2,1,0:T(8,128)(2,1)S(1)} async-done(((bf16[2,32,1024]{2,1,0:T(8,128)(2,1)}), bf16[2,32,1024]{2,1,0:T(8,128)(2,1)S(1)}, u32[]{:S(2)}, u32[]{:S(2)}) %all-to-all-start) | async-done | bytes 131104 | tf_op jit(solution)/shard_map/all_to_all | solution.py:17
  14.6 0.9 fusion.14
  15.5 0.7 multiply_reduce_fusion.2
  16.2 0.2 fusion.2
  16.4 0.1 copy.43
  16.5 0.6 copy.37
  17.1 4.9 %all-to-all-start.1 = ((bf16[8,1,9]{2,1,0:T(2,128)(2,1)}), bf16[8,1,9]{2,1,0:T(2,128)(2,1)S(1)}, u32[]{:S(2)}, u32[]{:S(2)}) async-start(bf16[8,1,9]{2,1,0:T(2,128)(2,1)} %copy.37), calls=%async_computation.1 | async-start | bytes 8192 | tf_op jit(solution)/shard_map/all_to_all | solution.py:45
  22.0 1.1 convolution_convert_fusion
  23.1 4.2 %all-to-all-done.1 = bf16[8,1,9]{2,1,0:T(2,128)(2,1)S(1)} async-done(((bf16[8,1,9]{2,1,0:T(2,128)(2,1)}), bf16[8,1,9]{2,1,0:T(2,128)(2,1)S(1)}, u32[]{:S(2)}, u32[]{:S(2)}) %all-to-all-start.1) | async-done | bytes 176 | tf_op jit(solution)/shard_map/all_to_all | solution.py:45
  27.3 3.5 %all-to-all-start.2 = ((bf16[8,9,2048]{2,1,0:T(8,128)(2,1)}), bf16[8,9,2048]{2,1,0:T(8,128)(2,1)S(1)}, u32[]{:S(2)}, u32[]{:S(2)}) async-start(bf16[8,9,2048]{2,1,0:T(8,128)(2,1)} %convolution_convert_fusion), calls=%async_computation.2 | async-start | bytes 1048576 | tf_op jit(solution)/shard_map/all_to_all | solution.py:44
  30.9 10.3 %all-to-all-done.2 = bf16[8,9,2048]{2,1,0:T(8,128)(2,1)S(1)} async-done(((bf16[8,9,2048]{2,1,0:T(8,128)(2,1)}), bf16[8,9,2048]{2,1,0:T(8,128)(2,1)S(1)}, u32[]{:S(2)}, u32[]{:S(2)}) %all-to-all-start.2) | async-done | bytes 294944 | tf_op jit(solution)/shard_map/all_to_all | solution.py:44
  41.2 0.1 reshape.60
  41.3 0.8 multiply_convert_fusion.1
  42.3 15.7 %fusion = (f32[72]{0:T(128)S(1)}, bf16[1,72,7680]{2,1,0:T(8,128)(2,1)}) fusion(bf16[1,72,7680]{2,1,0:T(8,128)(2,1)S(1)} %copy-done.1, f32[72]{0:T(128)S(1)} %reshape.61, bf16[72,2048]{1,0:T(8,128)(2,1)S(1)} %reshape.60, bf16[7680,2048]{1,0:T(8,128)(2,1)} %param.9), kind=kOutput, calls=%fused_computation.5 | convolution fusion | flops 2267688960 | bytes 33964608 | tf_op jit(solution)/shard_map/dot_general | solution.py:51
  58.1 11.7 %all_to_all.61 = f32[8,1,9]{2,1,0:T(1,128)S(1)} all-to-all(f32[8,1,9]{2,1,0:T(1,128)S(1)} %bitcast.55), channel_id=1, replica_groups=mesh['dp'=4,'expert'=4,'tensor'=2] {'expert','tensor'}, dimensions={0} | all-to-all | bytes 576 | tf_op jit(solution)/shard_map/all_to_all | solution.py:58
  70.1 0.8 convolution_bitcast_fusion
  70.9 0.3 all_to_all.50
  71.2 1.1 copy.39
  72.3 6.7 %all-to-all-start.3 = ((bf16[72,4,1920]{2,0,1:T(8,128)(2,1)}), bf16[72,4,1920]{2,0,1:T(8,128)(2,1)S(1)}, u32[]{:S(2)}, u32[]{:S(2)}) async-start(bf16[72,4,1920]{2,0,1:T(8,128)(2,1)} %copy.39), calls=%async_computation.3 | async-start | bytes 2211840 | tf_op jit(solution)/shard_map/all_to_all | solution.py:74
  79.0 1.0 convolution_convert_fusion.1
  80.0 13.6 %all-to-all-done.3 = bf16[72,4,1920]{2,0,1:T(8,128)(2,1)S(1)} async-done(((bf16[72,4,1920]{2,0,1:T(8,128)(2,1)}), bf16[72,4,1920]{2,0,1:T(8,128)(2,1)S(1)}, u32[]{:S(2)}, u32[]{:S(2)}) %all-to-all-start.3) | async-done | bytes 1105952 | tf_op jit(solution)/shard_map/all_to_all | solution.py:74
  93.6 8.0 %convert_bitcast_fusion = bf16[1920,2048]{0,1:T(8,128)(2,1)} fusion(bf16[288,2048]{1,0:T(8,128)(2,1)} %all-gather.4.cloned.1.call-done, bf16[288,1920]{1,0:T(8,128)(2,1)S(1)} %bitcast.51), kind=kOutput, calls=%fused_computation | convolution fusion | flops 2268856320 | bytes 10149888 | tf_op jit(solution)/shard_map/dot_general | solution.py:76
  101.6 10.6 %copy.41 = bf16[1920,2048]{1,0:T(8,128)(2,1)} copy(bf16[1920,2048]{0,1:T(8,128)(2,1)} %convert_bitcast_fusion) | data formatting | bytes 15728640
  112.2 15.5 %all-gather.6.cloned.1.call-done = f32[65536,8]{0,1:T(8,128)} async-done(((f32[2048,8]{0,1:T(8,128)}), f32[65536,8]{0,1:T(8,128)}) %all-gather.6.cloned.1.call-update) | async-done | bytes 2097168 | tf_op jit(solution)/shard_map/all_gather | solution.py:72
  127.7 2.3 %reduce_sum.76 = f32[2048,8]{0,1:T(8,128)} reduce(f32[32,2048,8]{1,2,0:T(8,128)} %bitcast.48, f32[]{:T(128)} %constant.9.clone.1), dimensions={0}, to_apply=%region_7.8 | reduce | flops 507904 | bytes 2162692 | tf_op jit(solution)/shard_map/reduce_sum | solution.py:73
  (29 shorter events, 0.8 us)
Async XLA Ops:
  7.2 14.8 %copy-start = (bf16[32,2048]{1,0:T(8,128)(2,1)S(1)}, bf16[32,2048]{1,0:T(8,128)(2,1)}, u32[]{:S(2)}) copy-start(bf16[32,2048]{1,0:T(8,128)(2,1)} %param.11) | copy-start | bytes 393220
  7.2 7.4 %all-to-all-start = ((bf16[2,32,1024]{2,1,0:T(8,128)(2,1)}), bf16[2,32,1024]{2,1,0:T(8,128)(2,1)S(1)}, u32[]{:S(2)}, u32[]{:S(2)}) async-start(bf16[2,32,1024]{2,1,0:T(8,128)(2,1)} %bitcast.53), calls=%async_computation | async-start | bytes 262144 | tf_op jit(solution)/shard_map/all_to_all | solution.py:17
  12.3 30.0 %copy-start.1 = (bf16[1,72,7680]{2,1,0:T(8,128)(2,1)S(1)}, bf16[1,72,7680]{2,1,0:T(8,128)(2,1)}, u32[]{:S(2)}) copy-start(bf16[1,72,7680]{2,1,0:T(8,128)(2,1)} %param.10) | copy-start | bytes 3317764
  17.1 10.1 %all-to-all-start.1 = ((bf16[8,1,9]{2,1,0:T(2,128)(2,1)}), bf16[8,1,9]{2,1,0:T(2,128)(2,1)S(1)}, u32[]{:S(2)}, u32[]{:S(2)}) async-start(bf16[8,1,9]{2,1,0:T(2,128)(2,1)} %copy.37), calls=%async_computation.1 | async-start | bytes 8192 | tf_op jit(solution)/shard_map/all_to_all | solution.py:45
  27.3 13.9 %all-to-all-start.2 = ((bf16[8,9,2048]{2,1,0:T(8,128)(2,1)}), bf16[8,9,2048]{2,1,0:T(8,128)(2,1)S(1)}, u32[]{:S(2)}, u32[]{:S(2)}) async-start(bf16[8,9,2048]{2,1,0:T(8,128)(2,1)} %convolution_convert_fusion), calls=%async_computation.2 | async-start | bytes 1048576 | tf_op jit(solution)/shard_map/all_to_all | solution.py:44
  30.8 62.8 %all-gather.4.cloned.1.call-start = ((), (), s32[]{:S(2)}) async-start(), calls=%async_computation.5 | async-start | bytes 1474560 | tf_op jit(solution)/shard_map/all_gather | solution.py:75
  42.2 27.8 %copy-start.3 = (s32[32,2]{0,1:T(2,128)S(1)}, s32[32,2]{0,1:T(2,128)}, u32[]{:S(2)}) copy-start(s32[32,2]{0,1:T(2,128)} %param.8) | copy-start | bytes 772
  42.2 85.5 %all-gather.6.cloned.1.call-start = ((), (), s32[]{:S(2)}) async-start(), calls=%async_computation.6 | async-start | bytes 2162688 | tf_op jit(solution)/shard_map/all_gather | solution.py:72
  71.2 7.8 %copy-start.2 = (bf16[2048,8]{0,1:T(8,128)(2,1)S(1)}, bf16[2048,8]{0,1:T(8,128)(2,1)}, u32[]{:S(2)}) copy-start(bf16[2048,8]{0,1:T(8,128)(2,1)} %param.7) | copy-start | bytes 98308
  72.3 21.3 %all-to-all-start.3 = ((bf16[72,4,1920]{2,0,1:T(8,128)(2,1)}), bf16[72,4,1920]{2,0,1:T(8,128)(2,1)S(1)}, u32[]{:S(2)}, u32[]{:S(2)}) async-start(bf16[72,4,1920]{2,0,1:T(8,128)(2,1)} %copy.39), calls=%async_computation.3 | async-start | bytes 2211840 | tf_op jit(solution)/shard_map/all_to_all | solution.py:74
Sparse Core Ops, SparseCore 0:
  42.3 21.1 all-gather.3
  71.0 56.6 all-gather.5
